TPU v7x, 256 devices: a whole 4x4x8 slice. The times are simulated.
256 devices in a mesh: row: 8 (over x, z_lo), col: 32 (over z_hi, y, core).
Axes of the slice: x: 4, y: 4, z: 8 (z_hi: 4, z_lo: 2; z = z_hi * 2 + z_lo), core: 2. Of those that a mesh axis runs over, the one named last changes fastest.
Arguments:
- tile_values: float32 [8, 32, 64, 128, 128], P('row', 'col'), may hold values from -0.15625 to 0.15625
- tile_rows: int32 [8, 32, 64], P('row', 'col'), may hold values from 0 to 159, as said below
- tile_cols: int32 [8, 32, 64], P('row', 'col'), may hold values from 0 to 23
- x_start: float32 [768, 128], P('col', 'row'), may hold values from -6 to 6
- z_start: float32 [1280, 128], P('row'), may hold values from -6 to 6
- y_start: float32 [1280, 128], P('row'), may hold values from -3 to 3
- lower_bound: float32 [1280, 128], P('row'), may hold values from -1.5 to -0.1
- upper_bound: float32 [1280, 128], P('row'), may hold values from 0.1 to 1.5
- cost_diag: float32 [768, 128], P('col', 'row'), may hold values from 0.1 to 10
- linear: float32 [768, 128], P('col', 'row'), may hold values from -6 to 6
- penalty: float32 [1], replicated, may hold values from 0.3 to 3
- proximal: float32 [1], replicated, may hold values from 0.1 to 1
- relaxation: float32 [1], replicated, may hold values from 1.2 to 1.8
Outputs:
- x_next: float32 [768, 128], P('col', 'row')
- z_next: float32 [1280, 128], P('row')
- y_next: float32 [1280, 128], P('row')
Inputs may be any that keep to these rules, and one draw needn't show every extreme that they name: On each device the 64 pairs (tile_rows, tile_cols) are distinct.
All inputs are finite; a program needn't handle non-finite values.
Results may differ from a plain program's by a relative error of at most 0.0002.
Values sent between devices are 32-bit elements; how exact they have to be, the bound alone decides.
A program may use at most 64 MiB of HBM per device.

v0:
```python
import jax
import jax.numpy as jnp
from jax import lax
from jax.sharding import PartitionSpec as P

ADMM_ITERS = 2
HIGH = lax.Precision.HIGHEST


def total_of_pieces(array, axis):
    return lax.all_gather(array, axis).sum(0)


def from_everyone(array, axis):
    copies = jnp.broadcast_to(array, (lax.axis_size(axis), *array.shape))
    return lax.all_to_all(copies, axis, split_axis=0, concat_axis=0, tiled=True)


def of_everyone(array, axis):
    everything = from_everyone(array, axis)
    return jnp.sum(everything, axis=0)


def turned_gather(arrays, axis, dims):
    turned = [jnp.moveaxis(a, dim, 0) for a, dim in zip(arrays, dims)]
    widths = [t[0].size for t in turned]
    both = jnp.concatenate([t.reshape(-1, w) for t, w in zip(turned, widths)], axis=1)
    out = lax.all_gather(both, axis, axis=0, tiled=True)
    parts = jnp.split(out, [sum(widths[:k]) for k in range(1, len(widths))], axis=1)
    return tuple(
        (
            jnp.moveaxis(b.reshape(-1, *t.shape[1:]), 0, dim)
            for b, t, dim in zip(parts, turned, dims)
        )
    )


def shards(
    tile_values,
    tile_rows,
    tile_cols,
    x_start,
    z_start,
    y_start,
    lower_bound,
    upper_bound,
    cost_diag,
    linear,
    penalty,
    proximal,
    relaxation,
):
    order_size = tile_values.shape[3]
    flat_tiles = tile_values.reshape(-1, order_size, order_size)
    row_index = tile_rows.reshape(-1)
    col_index = tile_cols.reshape(-1)
    count_tiles = row_index.shape[0]
    block_rows = z_start.shape[0]
    block_cols = x_start.shape[0]
    row_table = (
        lax.broadcasted_iota(jnp.int32, (block_rows, count_tiles), 0) == row_index[None, :]
    ).astype(jnp.float32)
    col_table = (
        lax.broadcasted_iota(jnp.int32, (block_cols, count_tiles), 0) == col_index[None, :]
    ).astype(jnp.float32)
    rho_value = penalty[0]
    sigma_value = proximal[0]
    relax_value = relaxation[0]
    empty_rows = jnp.zeros((block_rows, order_size), jnp.float32)

    def forward_terms(segment):
        piece_width = segment.shape[1]
        picked = jnp.take(segment, col_index, axis=0)
        products = jnp.einsum("kij,kj->ki", flat_tiles, picked, precision=HIGH)
        return jnp.dot(row_table, products, precision=HIGH)

    def apply_forward(vector):
        local_part = forward_terms(vector)
        return total_of_pieces(local_part, "col")

    def apply_backward(weights_rows):
        picked = jnp.take(weights_rows, row_index, axis=0)
        products = jnp.einsum("kij,ki->kj", flat_tiles, picked, precision=HIGH)
        local_part = jnp.dot(col_table, products, precision=HIGH)
        return of_everyone(local_part, "row")

    def global_totals(values):
        stacked = jnp.stack([jnp.sum(value) for value in values])
        return of_everyone(stacked, "col")

    x_now, diag_now, linear_now = turned_gather((x_start, cost_diag, linear), "row", (1, 1, 1))
    z_now, y_now = (z_start, y_start)
    image_now = empty_rows
    for outer_round in range(ADMM_ITERS):
        if outer_round == 0:
            image_now = apply_forward(x_now)
        target = rho_value * z_now - y_now - rho_value * image_now
        residual = -linear_now - diag_now * x_now + apply_backward(target)
        guess = x_now
        direction = residual
        image_sum = image_now
        norm_now = jnp.float32(1.0)
        norm_now = global_totals([residual * residual])[0]
        pushed = apply_forward(direction)
        applied = (diag_now + sigma_value) * direction + rho_value * apply_backward(pushed)
        curvature = global_totals([direction * applied])[0]
        step_length = norm_now / curvature
        guess = guess + step_length * direction
        image_sum = image_sum + step_length * pushed
        residual = residual - step_length * applied
        image_now = relax_value * image_sum + (1.0 - relax_value) * image_now
        x_now = relax_value * guess + (1.0 - relax_value) * x_now
        mixed = relax_value * image_sum + (1.0 - relax_value) * z_now
        z_fresh = jnp.minimum(jnp.maximum(mixed + y_now / rho_value, lower_bound), upper_bound)
        y_now = y_now + rho_value * (mixed - z_fresh)
        z_now = z_fresh
    piece_width = x_start.shape[1]
    x_now = lax.dynamic_slice_in_dim(x_now, lax.axis_index("row") * piece_width, piece_width, 1)
    return (x_now, z_now, y_now)


def solution(mesh):
    placed = (
        P("row", "col", None, None, None),
        P("row", "col", None),
        P("row", "col", None),
        P("col", "row"),
        P("row", None),
        P("row", None),
        P("row", None),
        P("row", None),
        P("col", "row"),
        P("col", "row"),
        P(),
        P(),
        P(),
    )
    return jax.shard_map(
        shards,
        mesh=mesh,
        in_specs=placed,
        out_specs=(P("col", "row"), P("row", None), P("row", None)),
        check_vma=False,
    )
```

profile of v0, /device:TPU:1, one launch (start us, length us, event | category | flops | bytes accessed | tf_op | source)
XLA Modules:
  0.0 375.3 jit_solution(2561918909377386901)
XLA Ops:
  7.2 0.7 compare_select_fusion.1
  7.9 0.7 compare_and_fusion.1
  8.6 0.8 pad_maximum_fusion
  9.4 23.0 %all_gather.21 = f32[128,72]{1,0:T(8,128)S(1)} all-gather(f32[16,72]{1,0:T(8,128)S(1)} %pad_maximum_fusion), channel_id=1, replica_groups=mesh['row'=8,'col'=32] {'row'}, dimensions={0}, use_global_device_ids=true | all-gather | bytes 41472 | tf_op jit(solution)/shard_map/all_gather | solution.py:28
  33.3 8.3 %fusion.12 = f32[64,1,128]{2,1,0:T(1,128)S(1)} fusion(f32[64,128,1]{1,2,0:T(1,128)S(1)} %bitcast.125, f32[1,1,64,128,128]{4,3,2,1,0:T(8,128)} %param.17), kind=kOutput, calls=%fused_computation.19 | convolution fusion | flops 12582912 | bytes 4259840 | tf_op jit(solution)/shard_map/kij,kj->ki/dot_general | solution.py:74
  41.6 0.8 fusion.16
  43.2 63.6 %all-gather.7.cloned.1.call-done = f32[5120,128]{1,0:T(8,128)} async-done(((f32[160,128]{1,0:T(8,128)}), f32[5120,128]{1,0:T(8,128)}) %all-gather.7.cloned.1.call-update) | async-done | bytes 2621456 | tf_op jit(solution)/shard_map/all_gather | solution.py:11
  106.7 1.9 reduce_sum.135
  109.3 5.3 %fusion.10 = f32[64,1,128]{2,1,0:T(1,128)S(1)} fusion(f32[64,128,1]{1,2,0:T(1,128)S(1)} %bitcast.126, f32[1,1,64,128,128]{4,3,2,1,0:T(8,128)} %param.17), kind=kOutput, calls=%fused_computation.17 | convolution fusion | flops 12582912 | bytes 4259840 | tf_op jit(solution)/shard_map/kij,ki->kj/dot_general | solution.py:83
  114.7 0.6 broadcast_in_dim.42
  115.4 4.0 %all-to-all-start = ((f32[8,24,128]{2,1,0:T(8,128)}), f32[8,24,128]{2,1,0:T(8,128)S(1)}, u32[]{:S(2)}, u32[]{:S(2)}) async-start(f32[8,24,128]{2,1,0:T(8,128)} %broadcast_in_dim.42), calls=%async_computation | async-start | bytes 196608 | tf_op jit(solution)/shard_map/all_to_all | solution.py:16
  119.5 5.2 %all-to-all-done = f32[8,24,128]{2,1,0:T(8,128)S(1)} async-done(((f32[8,24,128]{2,1,0:T(8,128)}), f32[8,24,128]{2,1,0:T(8,128)S(1)}, u32[]{:S(2)}, u32[]{:S(2)}) %all-to-all-start) | async-done | bytes 98336 | tf_op jit(solution)/shard_map/all_to_all | solution.py:16
  125.5 8.3 %fusion.8 = f32[64,1,128]{2,1,0:T(1,128)S(1)} fusion(f32[64,128,1]{1,2,0:T(1,128)S(1)} %bitcast.128, f32[1,1,64,128,128]{4,3,2,1,0:T(8,128)} %param.17), kind=kOutput, calls=%fused_computation.15 | convolution fusion | flops 12582912 | bytes 4259840 | tf_op jit(solution)/shard_map/kij,kj->ki/dot_general | solution.py:74
  133.8 0.8 fusion.15
  134.6 52.7 %all-gather.9.cloned.1.call-done = f32[5120,128]{1,0:T(8,128)} async-done(((f32[160,128]{1,0:T(8,128)}), f32[5120,128]{1,0:T(8,128)}) %all-gather.9.cloned.1.call-update) | async-done | bytes 2621456 | tf_op jit(solution)/shard_map/all_gather | solution.py:11
  187.3 1.9 reduce_sum.139
  189.8 5.3 %fusion.6 = f32[64,1,128]{2,1,0:T(1,128)S(1)} fusion(f32[64,128,1]{1,2,0:T(1,128)S(1)} %bitcast.129, f32[1,1,64,128,128]{4,3,2,1,0:T(8,128)} %param.17), kind=kOutput, calls=%fused_computation.13 | convolution fusion | flops 12582912 | bytes 4259840 | tf_op jit(solution)/shard_map/kij,ki->kj/dot_general | solution.py:83
  195.3 0.6 broadcast_in_dim.44
  195.9 4.0 %all-to-all-start.2 = ((f32[8,24,128]{2,1,0:T(8,128)}), f32[8,24,128]{2,1,0:T(8,128)S(1)}, u32[]{:S(2)}, u32[]{:S(2)}) async-start(f32[8,24,128]{2,1,0:T(8,128)} %broadcast_in_dim.44), calls=%async_computation.2 | async-start | bytes 196608 | tf_op jit(solution)/shard_map/all_to_all | solution.py:16
  200.5 4.7 %all-to-all-done.2 = f32[8,24,128]{2,1,0:T(8,128)S(1)} async-done(((f32[8,24,128]{2,1,0:T(8,128)}), f32[8,24,128]{2,1,0:T(8,128)S(1)}, u32[]{:S(2)}, u32[]{:S(2)}) %all-to-all-start.2) | async-done | bytes 98336 | tf_op jit(solution)/shard_map/all_to_all | solution.py:16
  205.9 0.7 broadcast_in_dim.43
  206.6 16.7 %all_to_all.44 = f32[32,1,1]{2,1,0:T(1,128)S(1)} all-to-all(f32[32,1,1]{2,1,0:T(1,128)S(1)} %broadcast_in_dim.43), channel_id=1, replica_groups=mesh['row'=8,'col'=32] {'col'}, dimensions={0} | all-to-all | bytes 256 | tf_op jit(solution)/shard_map/all_to_all | solution.py:16
  223.2 1.3 broadcast_in_dim.45
  224.5 4.1 %all-to-all-start.3 = ((f32[32,1,1]{2,1,0:T(1,128)}), f32[32,1,1]{2,1,0:T(1,128)S(1)}, u32[]{:S(2)}, u32[]{:S(2)}) async-start(f32[32,1,1]{2,1,0:T(1,128)} %broadcast_in_dim.45), calls=%async_computation.3 | async-start | bytes 32768 | tf_op jit(solution)/shard_map/all_to_all | solution.py:16
  229.5 0.6 reduce_sum.138
  230.2 7.9 %all-to-all-done.3 = f32[32,1,1]{2,1,0:T(1,128)S(1)} async-done(((f32[32,1,1]{2,1,0:T(1,128)}), f32[32,1,1]{2,1,0:T(1,128)S(1)}, u32[]{:S(2)}, u32[]{:S(2)}) %all-to-all-start.3) | async-done | bytes 160 | tf_op jit(solution)/shard_map/all_to_all | solution.py:16
  238.1 0.6 reduce_sum.142
  240.8 5.3 %fusion.4 = f32[64,1,128]{2,1,0:T(1,128)S(1)} fusion(f32[64,128,1]{1,2,0:T(1,128)S(1)} %bitcast.131, f32[1,1,64,128,128]{4,3,2,1,0:T(8,128)} %param.17), kind=kOutput, calls=%fused_computation.11 | convolution fusion | flops 12582912 | bytes 4259840 | tf_op jit(solution)/shard_map/kij,ki->kj/dot_general | solution.py:83
  246.3 7.8 %all_to_all.45 = f32[8,24,128]{2,1,0:T(8,128)S(1)} all-to-all(f32[8,24,128]{2,1,0:T(8,128)S(1)} %broadcast_in_dim.46), channel_id=1, replica_groups=mesh['row'=8,'col'=32] {'row'}, dimensions={0} | all-to-all | bytes 196608 | tf_op jit(solution)/shard_map/all_to_all | solution.py:16
  254.8 8.3 %fusion.2 = f32[64,1,128]{2,1,0:T(1,128)S(1)} fusion(f32[64,128,1]{1,2,0:T(1,128)S(1)} %bitcast.123, f32[1,1,64,128,128]{4,3,2,1,0:T(8,128)} %param.17), kind=kOutput, calls=%fused_computation.9 | convolution fusion | flops 12582912 | bytes 4259840 | tf_op jit(solution)/shard_map/kij,kj->ki/dot_general | solution.py:74
  263.1 0.8 fusion.14
  263.9 49.7 %all-gather.11.cloned.1.call-done = f32[5120,128]{1,0:T(8,128)} async-done(((f32[160,128]{1,0:T(8,128)}), f32[5120,128]{1,0:T(8,128)}) %all-gather.11.cloned.1.call-update) | async-done | bytes 2621456 | tf_op jit(solution)/shard_map/all_gather | solution.py:11
  313.7 1.9 reduce_sum.146
  316.2 5.3 %fusion = f32[64,1,128]{2,1,0:T(1,128)S(1)} fusion(f32[64,128,1]{1,2,0:T(1,128)S(1)} %bitcast.124, f32[1,1,64,128,128]{4,3,2,1,0:T(8,128)} %param.17), kind=kOutput, calls=%fused_computation.7 | convolution fusion | flops 12582912 | bytes 4259840 | tf_op jit(solution)/shard_map/kij,ki->kj/dot_general | solution.py:83
  321.6 0.6 broadcast_in_dim.48
  322.3 4.0 %all-to-all-start.6 = ((f32[8,24,128]{2,1,0:T(8,128)}), f32[8,24,128]{2,1,0:T(8,128)S(1)}, u32[]{:S(2)}, u32[]{:S(2)}) async-start(f32[8,24,128]{2,1,0:T(8,128)} %broadcast_in_dim.48), calls=%async_computation.6 | async-start | bytes 196608 | tf_op jit(solution)/shard_map/all_to_all | solution.py:16
  326.3 5.4 %all-to-all-done.6 = f32[8,24,128]{2,1,0:T(8,128)S(1)} async-done(((f32[8,24,128]{2,1,0:T(8,128)}), f32[8,24,128]{2,1,0:T(8,128)S(1)}, u32[]{:S(2)}, u32[]{:S(2)}) %all-to-all-start.6) | async-done | bytes 98336 | tf_op jit(solution)/shard_map/all_to_all | solution.py:16
  331.7 0.7 multiply_reduce_fusion
  332.4 1.3 broadcast_in_dim.47
  333.7 7.5 %all-to-all-start.5 = ((f32[32,1,1]{2,1,0:T(1,128)}), f32[32,1,1]{2,1,0:T(1,128)S(1)}, u32[]{:S(2)}, u32[]{:S(2)}) async-start(f32[32,1,1]{2,1,0:T(1,128)} %broadcast_in_dim.47), calls=%async_computation.5 | async-start | bytes 32768 | tf_op jit(solution)/shard_map/all_to_all | solution.py:16
  341.2 9.3 %all-to-all-done.5 = f32[32,1,1]{2,1,0:T(1,128)S(1)} async-done(((f32[32,1,1]{2,1,0:T(1,128)}), f32[32,1,1]{2,1,0:T(1,128)S(1)}, u32[]{:S(2)}, u32[]{:S(2)}) %all-to-all-start.5) | async-done | bytes 160 | tf_op jit(solution)/shard_map/all_to_all | solution.py:16
  350.5 1.3 broadcast_in_dim.49
  351.7 4.1 %all-to-all-start.7 = ((f32[32,1,1]{2,1,0:T(1,128)}), f32[32,1,1]{2,1,0:T(1,128)S(1)}, u32[]{:S(2)}, u32[]{:S(2)}) async-start(f32[32,1,1]{2,1,0:T(1,128)} %broadcast_in_dim.49), calls=%async_computation.7 | async-start | bytes 32768 | tf_op jit(solution)/shard_map/all_to_all | solution.py:16
  355.9 0.6 reduce_sum.145
  356.5 8.8 %all-to-all-done.7 = f32[32,1,1]{2,1,0:T(1,128)S(1)} async-done(((f32[32,1,1]{2,1,0:T(1,128)}), f32[32,1,1]{2,1,0:T(1,128)S(1)}, u32[]{:S(2)}, u32[]{:S(2)}) %all-to-all-start.7) | async-done | bytes 160 | tf_op jit(solution)/shard_map/all_to_all | solution.py:16
  365.3 0.6 reduce_sum.149
  367.4 0.7 copy.35
  368.0 0.7 multiply_add_fusion
  (55 shorter events, 6.8 us)
Async XLA Ops:
  7.2 34.5 %copy-start.5 = (s32[1,1,64]{2,1,0:T(1,128)S(1)}, s32[1,1,64]{2,1,0:T(1,128)}, u32[]{:S(2)}) copy-start(s32[1,1,64]{2,1,0:T(1,128)} %param.18) | copy-start | bytes 772
  7.2 101.4 %copy-start.1 = (f32[160,128]{1,0:T(8,128)S(1)}, f32[160,128]{1,0:T(8,128)}, u32[]{:S(2)}) copy-start(f32[160,128]{1,0:T(8,128)} %param.21) | copy-start | bytes 245764
  7.2 101.4 %copy-start = (f32[160,128]{1,0:T(8,128)S(1)}, f32[160,128]{1,0:T(8,128)}, u32[]{:S(2)}) copy-start(f32[160,128]{1,0:T(8,128)} %param.22) | copy-start | bytes 245764
  7.2 99.5 %all-gather.7.cloned.1.call-start = ((), (), s32[]{:S(2)}) async-start(), calls=%async_computation.8 | async-start | bytes 2703360 | tf_op jit(solution)/shard_map/all_gather | solution.py:11
  41.6 73.0 %copy-start.4 = (s32[1,1,64]{2,1,0:T(1,128)S(1)}, s32[1,1,64]{2,1,0:T(1,128)}, u32[]{:S(2)}) copy-start(s32[1,1,64]{2,1,0:T(1,128)} %param.19) | copy-start | bytes 772
  115.4 9.4 %all-to-all-start = ((f32[8,24,128]{2,1,0:T(8,128)}), f32[8,24,128]{2,1,0:T(8,128)S(1)}, u32[]{:S(2)}, u32[]{:S(2)}) async-start(f32[8,24,128]{2,1,0:T(8,128)} %broadcast_in_dim.42), calls=%async_computation | async-start | bytes 196608 | tf_op jit(solution)/shard_map/all_to_all | solution.py:16
  119.4 67.9 %all-gather.9.cloned.1.call-start = ((), (), s32[]{:S(2)}) async-start(), calls=%async_computation.9 | async-start | bytes 2703360 | tf_op jit(solution)/shard_map/all_gather | solution.py:11
  133.8 106.3 %copy-start.2 = (f32[160,128]{1,0:T(8,128)S(1)}, f32[160,128]{1,0:T(8,128)}, u32[]{:S(2)}) copy-start(f32[160,128]{1,0:T(8,128)} %param.24) | copy-start | bytes 245764
  133.8 106.3 %copy-start.3 = (f32[160,128]{1,0:T(8,128)S(1)}, f32[160,128]{1,0:T(8,128)}, u32[]{:S(2)}) copy-start(f32[160,128]{1,0:T(8,128)} %param.23) | copy-start | bytes 245764
  195.9 9.4 %all-to-all-start.2 = ((f32[8,24,128]{2,1,0:T(8,128)}), f32[8,24,128]{2,1,0:T(8,128)S(1)}, u32[]{:S(2)}, u32[]{:S(2)}) async-start(f32[8,24,128]{2,1,0:T(8,128)} %broadcast_in_dim.44), calls=%async_computation.2 | async-start | bytes 196608 | tf_op jit(solution)/shard_map/all_to_all | solution.py:16
  224.5 13.6 %all-to-all-start.3 = ((f32[32,1,1]{2,1,0:T(1,128)}), f32[32,1,1]{2,1,0:T(1,128)S(1)}, u32[]{:S(2)}, u32[]{:S(2)}) async-start(f32[32,1,1]{2,1,0:T(1,128)} %broadcast_in_dim.45), calls=%async_computation.3 | async-start | bytes 32768 | tf_op jit(solution)/shard_map/all_to_all | solution.py:16
  228.7 85.0 %all-gather.11.cloned.1.call-start = ((), (), s32[]{:S(2)}) async-start(), calls=%async_computation.10 | async-start | bytes 2703360 | tf_op jit(solution)/shard_map/all_gather | solution.py:11
  322.3 9.4 %all-to-all-start.6 = ((f32[8,24,128]{2,1,0:T(8,128)}), f32[8,24,128]{2,1,0:T(8,128)S(1)}, u32[]{:S(2)}, u32[]{:S(2)}) async-start(f32[8,24,128]{2,1,0:T(8,128)} %broadcast_in_dim.48), calls=%async_computation.6 | async-start | bytes 196608 | tf_op jit(solution)/shard_map/all_to_all | solution.py:16
  333.7 16.8 %all-to-all-start.5 = ((f32[32,1,1]{2,1,0:T(1,128)}), f32[32,1,1]{2,1,0:T(1,128)S(1)}, u32[]{:S(2)}, u32[]{:S(2)}) async-start(f32[32,1,1]{2,1,0:T(1,128)} %broadcast_in_dim.47), calls=%async_computation.5 | async-start | bytes 32768 | tf_op jit(solution)/shard_map/all_to_all | solution.py:16
  351.7 13.6 %all-to-all-start.7 = ((f32[32,1,1]{2,1,0:T(1,128)}), f32[32,1,1]{2,1,0:T(1,128)S(1)}, u32[]{:S(2)}, u32[]{:S(2)}) async-start(f32[32,1,1]{2,1,0:T(1,128)} %broadcast_in_dim.49), calls=%async_computation.7 | async-start | bytes 32768 | tf_op jit(solution)/shard_map/all_to_all | solution.py:16
Sparse Core Ops, SparseCore 0:
  42.6 64.0 all-gather.6
  134.7 52.4 all-gather.8
  264.0 49.5 all-gather.10
where the time goes:
time: 376 us; the launch traced here: 375 us
  waiting for transfers between devices  207 us (55%)
  matrix products  49.1 us (13%)
  blocking collectives  47.5 us (13%)
  starting transfers between devices  28 us (7%)
  between operations  18.6 us (5%)
  other arithmetic  13.1 us (3%)
  local copies, waits for them, and re-layouts  11.6 us (3%)
    all_gather x3, waiting for transfers between devices, total_of_pieces(): return lax.all_gather(array, axis).sum(0)  166 us
    all_to_all x6, waiting for transfers between devices, from_everyone(): return lax.all_to_all(copies, axis, split_axis=0, concat_axis=0, tiled=True)  41.4 us
    all_to_all x6, starting transfers between devices, from_everyone(): return lax.all_to_all(copies, axis, split_axis=0, concat_axis=0, tiled=True)  27.7 us
    dot_general x3, matrix products, forward_terms(): products = jnp.einsum('kij,kj->ki', flat_tiles, picked, precision=HIGH)  24.9 us
    all_to_all x2, blocking collectives, from_everyone(): return lax.all_to_all(copies, axis, split_axis=0, concat_axis=0, tiled=True)  24.4 us
    all_gather x1, blocking collectives, turned_gather(): out = lax.all_gather(both, axis, axis=0, tiled=True)  23 us
    dot_general x4, matrix products, apply_backward(): products = jnp.einsum('kij,ki->kj', flat_tiles, picked, precision=HIGH)  21.1 us
  transfers between devices with their start and end apart: 9, of which 9 were waited for; matrix products, arithmetic and copies ran while one was open for 0% of the time, Pallas kernels for 0%

commit v1 on v0

--- a/solution.py
+++ b/solution.py
@@ -5,6 +5,14 @@
 
 ADMM_ITERS = 2
 HIGH = lax.Precision.HIGHEST
+
+
+def lay_sums_all(xs, named_axis):
+    pile = []
+    for _ in range(lax.axis_size(named_axis)):
+        pile.append(xs)
+    front = lax.all_to_all(jnp.stack(pile), named_axis, 0, 0)
+    return jnp.concatenate(front, 0)
 
 
 def total_of_pieces(array, axis):
@@ -25,7 +33,7 @@
     turned = [jnp.moveaxis(a, dim, 0) for a, dim in zip(arrays, dims)]
     widths = [t[0].size for t in turned]
     both = jnp.concatenate([t.reshape(-1, w) for t, w in zip(turned, widths)], axis=1)
-    out = lax.all_gather(both, axis, axis=0, tiled=True)
+    out = lay_sums_all(both, axis)
     parts = jnp.split(out, [sum(widths[:k]) for k in range(1, len(widths))], axis=1)
     return tuple(
         (

time: 376 us -> 357 us (0.949)
  blocking collectives: 47.5 us -> 24.4 us
  starting transfers between devices: 28 us -> 34.2 us
    all_gather x1 -> x0, blocking collectives: 23 us -> none  [turned_gather(): out = lax.all_gather(both, axis, axis=0, tiled=True)]
    all_gather x3, waiting for transfers between devices: 166 us -> 159 us  [total_of_pieces(): return lax.all_gather(array, axis).sum(0)]
    all_to_all x0 -> x1, starting transfers between devices: none -> 6.19 us  [lay_sums_all(): front = lax.all_to_all(jnp.stack(pile), named_axis, 0, 0)]
    all_to_all x0 -> x1, waiting for transfers between devices: none -> 3.82 us  [lay_sums_all(): front = lax.all_to_all(jnp.stack(pile), named_axis, 0, 0)]
  transfers between devices with their start and end apart: 9 -> 10, of which waited for: 9 -> 10; matrix products, arithmetic and copies ran while one was open for 0% -> 1% of each run, Pallas kernels for 0% -> 0%
where the time goes in v1:
time: 357 us; the launch traced here: 356 us
  waiting for transfers between devices  205 us (57%)
  matrix products  49.1 us (14%)
  starting transfers between devices  34.2 us (10%)
  blocking collectives  24.4 us (7%)
  between operations  18.6 us (5%)
  other arithmetic  13.1 us (4%)
  local copies, waits for them, and re-layouts  12.2 us (3%)
    all_gather x3, waiting for transfers between devices, total_of_pieces(): return lax.all_gather(array, axis).sum(0)  159 us
    all_to_all x6, waiting for transfers between devices, from_everyone(): return lax.all_to_all(copies, axis, split_axis=0, concat_axis=0, tiled=True)  41.4 us
    all_to_all x6, starting transfers between devices, from_everyone(): return lax.all_to_all(copies, axis, split_axis=0, concat_axis=0, tiled=True)  27.7 us
    dot_general x3, matrix products, forward_terms(): products = jnp.einsum('kij,kj->ki', flat_tiles, picked, precision=HIGH)  24.9 us
    all_to_all x2, blocking collectives, from_everyone(): return lax.all_to_all(copies, axis, split_axis=0, concat_axis=0, tiled=True)  24.4 us
    dot_general x4, matrix products, apply_backward(): products = jnp.einsum('kij,ki->kj', flat_tiles, picked, precision=HIGH)  21.1 us
  transfers between devices with their start and end apart: 10, of which 10 were waited for; matrix products, arithmetic and copies ran while one was open for 1% of the time, Pallas kernels for 0%

profile of v1, /device:TPU:1, one launch (start us, length us, event | category | flops | bytes accessed | tf_op | source)
XLA Modules:
  0.0 356.3 jit_solution(8852839247714823892)
XLA Ops:
  7.2 0.8 pad_maximum_fusion
  8.0 0.6 stack.2
  8.7 6.2 %all-to-all-start = ((f32[8,16,72]{2,1,0:T(8,128)}), f32[8,16,72]{2,1,0:T(8,128)S(1)}, u32[]{:S(2)}, u32[]{:S(2)}) async-start(f32[8,16,72]{2,1,0:T(8,128)} %stack.2), calls=%async_computation | async-start | bytes 131072 | tf_op jit(solution)/shard_map/all_to_all | solution.py:14
  14.9 0.7 compare_select_fusion.1
  15.6 0.7 compare_and_fusion.1
  16.2 3.8 %all-to-all-done = f32[8,16,72]{2,1,0:T(8,128)S(1)} async-done(((f32[8,16,72]{2,1,0:T(8,128)}), f32[8,16,72]{2,1,0:T(8,128)S(1)}, u32[]{:S(2)}, u32[]{:S(2)}) %all-to-all-start) | async-done | bytes 36896 | tf_op jit(solution)/shard_map/all_to_all | solution.py:14
  20.9 8.3 %fusion.12 = f32[64,1,128]{2,1,0:T(1,128)S(1)} fusion(f32[64,128,1]{1,2,0:T(1,128)S(1)} %bitcast.127, f32[1,1,64,128,128]{4,3,2,1,0:T(8,128)} %param.17), kind=kOutput, calls=%fused_computation.19 | convolution fusion | flops 12582912 | bytes 4259840 | tf_op jit(solution)/shard_map/kij,kj->ki/dot_general | solution.py:82
  29.2 0.8 fusion.16
  30.8 57.0 %all-gather.7.cloned.1.call-done = f32[5120,128]{1,0:T(8,128)} async-done(((f32[160,128]{1,0:T(8,128)}), f32[5120,128]{1,0:T(8,128)}) %all-gather.7.cloned.1.call-update) | async-done | bytes 2621456 | tf_op jit(solution)/shard_map/all_gather | solution.py:19
  87.8 1.9 reduce_sum.135
  90.4 5.3 %fusion.10 = f32[64,1,128]{2,1,0:T(1,128)S(1)} fusion(f32[64,128,1]{1,2,0:T(1,128)S(1)} %bitcast.128, f32[1,1,64,128,128]{4,3,2,1,0:T(8,128)} %param.17), kind=kOutput, calls=%fused_computation.17 | convolution fusion | flops 12582912 | bytes 4259840 | tf_op jit(solution)/shard_map/kij,ki->kj/dot_general | solution.py:91
  95.8 0.6 broadcast_in_dim.42
  96.5 4.0 %all-to-all-start.1 = ((f32[8,24,128]{2,1,0:T(8,128)}), f32[8,24,128]{2,1,0:T(8,128)S(1)}, u32[]{:S(2)}, u32[]{:S(2)}) async-start(f32[8,24,128]{2,1,0:T(8,128)} %broadcast_in_dim.42), calls=%async_computation.1 | async-start | bytes 196608 | tf_op jit(solution)/shard_map/all_to_all | solution.py:24
  100.6 5.2 %all-to-all-done.1 = f32[8,24,128]{2,1,0:T(8,128)S(1)} async-done(((f32[8,24,128]{2,1,0:T(8,128)}), f32[8,24,128]{2,1,0:T(8,128)S(1)}, u32[]{:S(2)}, u32[]{:S(2)}) %all-to-all-start.1) | async-done | bytes 98336 | tf_op jit(solution)/shard_map/all_to_all | solution.py:24
  106.5 8.3 %fusion.8 = f32[64,1,128]{2,1,0:T(1,128)S(1)} fusion(f32[64,128,1]{1,2,0:T(1,128)S(1)} %bitcast.130, f32[1,1,64,128,128]{4,3,2,1,0:T(8,128)} %param.17), kind=kOutput, calls=%fused_computation.15 | convolution fusion | flops 12582912 | bytes 4259840 | tf_op jit(solution)/shard_map/kij,kj->ki/dot_general | solution.py:82
  114.8 0.8 fusion.15
  115.7 52.7 %all-gather.9.cloned.1.call-done = f32[5120,128]{1,0:T(8,128)} async-done(((f32[160,128]{1,0:T(8,128)}), f32[5120,128]{1,0:T(8,128)}) %all-gather.9.cloned.1.call-update) | async-done | bytes 2621456 | tf_op jit(solution)/shard_map/all_gather | solution.py:19
  168.4 1.9 reduce_sum.139
  170.9 5.3 %fusion.6 = f32[64,1,128]{2,1,0:T(1,128)S(1)} fusion(f32[64,128,1]{1,2,0:T(1,128)S(1)} %bitcast.131, f32[1,1,64,128,128]{4,3,2,1,0:T(8,128)} %param.17), kind=kOutput, calls=%fused_computation.13 | convolution fusion | flops 12582912 | bytes 4259840 | tf_op jit(solution)/shard_map/kij,ki->kj/dot_general | solution.py:91
  176.3 0.6 broadcast_in_dim.44
  177.0 4.0 %all-to-all-start.3 = ((f32[8,24,128]{2,1,0:T(8,128)}), f32[8,24,128]{2,1,0:T(8,128)S(1)}, u32[]{:S(2)}, u32[]{:S(2)}) async-start(f32[8,24,128]{2,1,0:T(8,128)} %broadcast_in_dim.44), calls=%async_computation.3 | async-start | bytes 196608 | tf_op jit(solution)/shard_map/all_to_all | solution.py:24
  181.6 4.7 %all-to-all-done.3 = f32[8,24,128]{2,1,0:T(8,128)S(1)} async-done(((f32[8,24,128]{2,1,0:T(8,128)}), f32[8,24,128]{2,1,0:T(8,128)S(1)}, u32[]{:S(2)}, u32[]{:S(2)}) %all-to-all-start.3) | async-done | bytes 98336 | tf_op jit(solution)/shard_map/all_to_all | solution.py:24
  187.0 0.7 broadcast_in_dim.43
  187.6 16.7 %all_to_all.49 = f32[32,1,1]{2,1,0:T(1,128)S(1)} all-to-all(f32[32,1,1]{2,1,0:T(1,128)S(1)} %broadcast_in_dim.43), channel_id=1, replica_groups=mesh['row'=8,'col'=32] {'col'}, dimensions={0} | all-to-all | bytes 256 | tf_op jit(solution)/shard_map/all_to_all | solution.py:24
  204.3 1.3 broadcast_in_dim.45
  205.6 4.1 %all-to-all-start.4 = ((f32[32,1,1]{2,1,0:T(1,128)}), f32[32,1,1]{2,1,0:T(1,128)S(1)}, u32[]{:S(2)}, u32[]{:S(2)}) async-start(f32[32,1,1]{2,1,0:T(1,128)} %broadcast_in_dim.45), calls=%async_computation.4 | async-start | bytes 32768 | tf_op jit(solution)/shard_map/all_to_all | solution.py:24
  210.6 0.6 reduce_sum.138
  211.2 7.9 %all-to-all-done.4 = f32[32,1,1]{2,1,0:T(1,128)S(1)} async-done(((f32[32,1,1]{2,1,0:T(1,128)}), f32[32,1,1]{2,1,0:T(1,128)S(1)}, u32[]{:S(2)}, u32[]{:S(2)}) %all-to-all-start.4) | async-done | bytes 160 | tf_op jit(solution)/shard_map/all_to_all | solution.py:24
  221.9 5.3 %fusion.4 = f32[64,1,128]{2,1,0:T(1,128)S(1)} fusion(f32[64,128,1]{1,2,0:T(1,128)S(1)} %bitcast.133, f32[1,1,64,128,128]{4,3,2,1,0:T(8,128)} %param.17), kind=kOutput, calls=%fused_computation.11 | convolution fusion | flops 12582912 | bytes 4259840 | tf_op jit(solution)/shard_map/kij,ki->kj/dot_general | solution.py:91
  227.3 7.8 %all_to_all.50 = f32[8,24,128]{2,1,0:T(8,128)S(1)} all-to-all(f32[8,24,128]{2,1,0:T(8,128)S(1)} %broadcast_in_dim.46), channel_id=1, replica_groups=mesh['row'=8,'col'=32] {'row'}, dimensions={0} | all-to-all | bytes 196608 | tf_op jit(solution)/shard_map/all_to_all | solution.py:24
  235.8 8.3 %fusion.2 = f32[64,1,128]{2,1,0:T(1,128)S(1)} fusion(f32[64,128,1]{1,2,0:T(1,128)S(1)} %bitcast.125, f32[1,1,64,128,128]{4,3,2,1,0:T(8,128)} %param.17), kind=kOutput, calls=%fused_computation.9 | convolution fusion | flops 12582912 | bytes 4259840 | tf_op jit(solution)/shard_map/kij,kj->ki/dot_general | solution.py:82
  244.1 0.8 fusion.14
  245.0 49.7 %all-gather.11.cloned.1.call-done = f32[5120,128]{1,0:T(8,128)} async-done(((f32[160,128]{1,0:T(8,128)}), f32[5120,128]{1,0:T(8,128)}) %all-gather.11.cloned.1.call-update) | async-done | bytes 2621456 | tf_op jit(solution)/shard_map/all_gather | solution.py:19
  294.7 1.9 reduce_sum.146
  297.3 5.3 %fusion = f32[64,1,128]{2,1,0:T(1,128)S(1)} fusion(f32[64,128,1]{1,2,0:T(1,128)S(1)} %bitcast.126, f32[1,1,64,128,128]{4,3,2,1,0:T(8,128)} %param.17), kind=kOutput, calls=%fused_computation.7 | convolution fusion | flops 12582912 | bytes 4259840 | tf_op jit(solution)/shard_map/kij,ki->kj/dot_general | solution.py:91
  303.4 4.0 %all-to-all-start.7 = ((f32[8,24,128]{2,1,0:T(8,128)}), f32[8,24,128]{2,1,0:T(8,128)S(1)}, u32[]{:S(2)}, u32[]{:S(2)}) async-start(f32[8,24,128]{2,1,0:T(8,128)} %broadcast_in_dim.48), calls=%async_computation.7 | async-start | bytes 196608 | tf_op jit(solution)/shard_map/all_to_all | solution.py:24
  307.3 5.4 %all-to-all-done.7 = f32[8,24,128]{2,1,0:T(8,128)S(1)} async-done(((f32[8,24,128]{2,1,0:T(8,128)}), f32[8,24,128]{2,1,0:T(8,128)S(1)}, u32[]{:S(2)}, u32[]{:S(2)}) %all-to-all-start.7) | async-done | bytes 98336 | tf_op jit(solution)/shard_map/all_to_all | solution.py:24
  312.7 0.7 multiply_reduce_fusion
  313.4 1.3 broadcast_in_dim.47
  314.7 7.5 %all-to-all-start.6 = ((f32[32,1,1]{2,1,0:T(1,128)}), f32[32,1,1]{2,1,0:T(1,128)S(1)}, u32[]{:S(2)}, u32[]{:S(2)}) async-start(f32[32,1,1]{2,1,0:T(1,128)} %broadcast_in_dim.47), calls=%async_computation.6 | async-start | bytes 32768 | tf_op jit(solution)/shard_map/all_to_all | solution.py:24
  322.2 9.3 %all-to-all-done.6 = f32[32,1,1]{2,1,0:T(1,128)S(1)} async-done(((f32[32,1,1]{2,1,0:T(1,128)}), f32[32,1,1]{2,1,0:T(1,128)S(1)}, u32[]{:S(2)}, u32[]{:S(2)}) %all-to-all-start.6) | async-done | bytes 160 | tf_op jit(solution)/shard_map/all_to_all | solution.py:24
  331.5 1.3 broadcast_in_dim.49
  332.8 4.1 %all-to-all-start.8 = ((f32[32,1,1]{2,1,0:T(1,128)}), f32[32,1,1]{2,1,0:T(1,128)S(1)}, u32[]{:S(2)}, u32[]{:S(2)}) async-start(f32[32,1,1]{2,1,0:T(1,128)} %broadcast_in_dim.49), calls=%async_computation.8 | async-start | bytes 32768 | tf_op jit(solution)/shard_map/all_to_all | solution.py:24
  336.9 0.6 reduce_sum.145
  337.6 8.8 %all-to-all-done.8 = f32[32,1,1]{2,1,0:T(1,128)S(1)} async-done(((f32[32,1,1]{2,1,0:T(1,128)}), f32[32,1,1]{2,1,0:T(1,128)S(1)}, u32[]{:S(2)}, u32[]{:S(2)}) %all-to-all-start.8) | async-done | bytes 160 | tf_op jit(solution)/shard_map/all_to_all | solution.py:24
  346.4 0.6 reduce_sum.149
  348.4 0.7 copy.33
  349.1 0.7 multiply_add_fusion
  (57 shorter events, 8.1 us)
Async XLA Ops:
  7.2 22.1 %copy-start.5 = (s32[1,1,64]{2,1,0:T(1,128)S(1)}, s32[1,1,64]{2,1,0:T(1,128)}, u32[]{:S(2)}) copy-start(s32[1,1,64]{2,1,0:T(1,128)} %param.18) | copy-start | bytes 772
  7.2 82.5 %copy-start.1 = (f32[160,128]{1,0:T(8,128)S(1)}, f32[160,128]{1,0:T(8,128)}, u32[]{:S(2)}) copy-start(f32[160,128]{1,0:T(8,128)} %param.21) | copy-start | bytes 245764
  7.2 82.5 %copy-start = (f32[160,128]{1,0:T(8,128)S(1)}, f32[160,128]{1,0:T(8,128)}, u32[]{:S(2)}) copy-start(f32[160,128]{1,0:T(8,128)} %param.22) | copy-start | bytes 245764
  8.7 11.4 %all-to-all-start = ((f32[8,16,72]{2,1,0:T(8,128)}), f32[8,16,72]{2,1,0:T(8,128)S(1)}, u32[]{:S(2)}, u32[]{:S(2)}) async-start(f32[8,16,72]{2,1,0:T(8,128)} %stack.2), calls=%async_computation | async-start | bytes 131072 | tf_op jit(solution)/shard_map/all_to_all | solution.py:14
  14.9 72.9 %all-gather.7.cloned.1.call-start = ((), (), s32[]{:S(2)}) async-start(), calls=%async_computation.9 | async-start | bytes 2703360 | tf_op jit(solution)/shard_map/all_gather | solution.py:19
  29.2 66.4 %copy-start.4 = (s32[1,1,64]{2,1,0:T(1,128)S(1)}, s32[1,1,64]{2,1,0:T(1,128)}, u32[]{:S(2)}) copy-start(s32[1,1,64]{2,1,0:T(1,128)} %param.19) | copy-start | bytes 772
  96.5 9.4 %all-to-all-start.1 = ((f32[8,24,128]{2,1,0:T(8,128)}), f32[8,24,128]{2,1,0:T(8,128)S(1)}, u32[]{:S(2)}, u32[]{:S(2)}) async-start(f32[8,24,128]{2,1,0:T(8,128)} %broadcast_in_dim.42), calls=%async_computation.1 | async-start | bytes 196608 | tf_op jit(solution)/shard_map/all_to_all | solution.py:24
  100.4 67.9 %all-gather.9.cloned.1.call-start = ((), (), s32[]{:S(2)}) async-start(), calls=%async_computation.10 | async-start | bytes 2703360 | tf_op jit(solution)/shard_map/all_gather | solution.py:19
  114.8 106.3 %copy-start.2 = (f32[160,128]{1,0:T(8,128)S(1)}, f32[160,128]{1,0:T(8,128)}, u32[]{:S(2)}) copy-start(f32[160,128]{1,0:T(8,128)} %param.24) | copy-start | bytes 245764
  114.8 106.3 %copy-start.3 = (f32[160,128]{1,0:T(8,128)S(1)}, f32[160,128]{1,0:T(8,128)}, u32[]{:S(2)}) copy-start(f32[160,128]{1,0:T(8,128)} %param.23) | copy-start | bytes 245764
  177.0 9.4 %all-to-all-start.3 = ((f32[8,24,128]{2,1,0:T(8,128)}), f32[8,24,128]{2,1,0:T(8,128)S(1)}, u32[]{:S(2)}, u32[]{:S(2)}) async-start(f32[8,24,128]{2,1,0:T(8,128)} %broadcast_in_dim.44), calls=%async_computation.3 | async-start | bytes 196608 | tf_op jit(solution)/shard_map/all_to_all | solution.py:24
  205.6 13.6 %all-to-all-start.4 = ((f32[32,1,1]{2,1,0:T(1,128)}), f32[32,1,1]{2,1,0:T(1,128)S(1)}, u32[]{:S(2)}, u32[]{:S(2)}) async-start(f32[32,1,1]{2,1,0:T(1,128)} %broadcast_in_dim.45), calls=%async_computation.4 | async-start | bytes 32768 | tf_op jit(solution)/shard_map/all_to_all | solution.py:24
  209.7 85.0 %all-gather.11.cloned.1.call-start = ((), (), s32[]{:S(2)}) async-start(), calls=%async_computation.11 | async-start | bytes 2703360 | tf_op jit(solution)/shard_map/all_gather | solution.py:19
  303.4 9.4 %all-to-all-start.7 = ((f32[8,24,128]{2,1,0:T(8,128)}), f32[8,24,128]{2,1,0:T(8,128)S(1)}, u32[]{:S(2)}, u32[]{:S(2)}) async-start(f32[8,24,128]{2,1,0:T(8,128)} %broadcast_in_dim.48), calls=%async_computation.7 | async-start | bytes 196608 | tf_op jit(solution)/shard_map/all_to_all | solution.py:24
  314.7 16.8 %all-to-all-start.6 = ((f32[32,1,1]{2,1,0:T(1,128)}), f32[32,1,1]{2,1,0:T(1,128)S(1)}, u32[]{:S(2)}, u32[]{:S(2)}) async-start(f32[32,1,1]{2,1,0:T(1,128)} %broadcast_in_dim.47), calls=%async_computation.6 | async-start | bytes 32768 | tf_op jit(solution)/shard_map/all_to_all | solution.py:24
  332.8 13.6 %all-to-all-start.8 = ((f32[32,1,1]{2,1,0:T(1,128)}), f32[32,1,1]{2,1,0:T(1,128)S(1)}, u32[]{:S(2)}, u32[]{:S(2)}) async-start(f32[32,1,1]{2,1,0:T(1,128)} %broadcast_in_dim.49), calls=%async_computation.8 | async-start | bytes 32768 | tf_op jit(solution)/shard_map/all_to_all | solution.py:24
Sparse Core Ops, SparseCore 0:
  30.2 57.5 all-gather.6
  115.8 52.4 all-gather.8
  245.1 49.5 all-gather.10
